TPU v7x, 32 devices: a whole 2x2x4 slice. The times are simulated.
32 devices in a mesh: dp: 8 (over y, x, core), mp: 4 (over z).
Axes of the slice: x: 2, y: 2, z: 4, core: 2. Of those that a mesh axis runs over, the one named last changes fastest.
Arguments:
- tokens: bfloat16 [4096, 1024], P('dp', 'mp'), may hold values from -150 to 150
- pre_gain: bfloat16 [1024], P('mp'), may hold values from 0.25 to 1.75
- input_weight: bfloat16 [3, 1024, 1024], P(None, 'dp', 'mp'), may hold values from -0.125 to 0.125
- output_weight: bfloat16 [1024, 1024], P('mp', 'dp'), may hold values from -1 to 1
- position_bias: bfloat16 [16, 512, 512], P('mp'), may hold values from -3 to 353
- post_gain: bfloat16 [1024], P('mp'), may hold values from 0.25 to 1.75
Outputs:
- stream: bfloat16 [4096, 1024], P('dp', 'mp')
- normed: bfloat16 [4096, 1024], P('dp', 'mp')
All inputs are finite; a program needn't handle non-finite values.
Results may differ from a plain program's by a relative error of at most 0.013.
Values may be sent and summed in bfloat16 or wider, within the bound.
A program may use at most 64 MiB of HBM per device.

v0:
```python
import jax
import jax.numpy as jnp
from jax import lax
from jax.sharding import PartitionSpec as P

epsilon = 1e-06


def attend_all(mixed_heads, position_bias):
    row_count = mixed_heads.shape[1]
    inner_width = mixed_heads.shape[2]
    head_count = position_bias.shape[0]
    seq_len = position_bias.shape[1]
    grouped = mixed_heads.reshape(
        3, row_count // seq_len, seq_len, head_count, inner_width // head_count
    )
    bias_wide = position_bias.astype(jnp.float32)

    def one_sequence(sequence):
        sequence_block = lax.dynamic_index_in_dim(grouped, sequence, 1, keepdims=False)
        scores = (
            jnp.einsum(
                "qhd,khd->hqk",
                sequence_block[0],
                sequence_block[1],
                preferred_element_type=jnp.float32,
            )
            + bias_wide
        )
        row_max = jnp.max(scores, axis=2, keepdims=True)
        weights = jnp.exp(scores - row_max)
        probabilities = (weights / jnp.sum(weights, axis=2, keepdims=True)).astype(jnp.bfloat16)
        context = jnp.einsum(
            "hqk,khd->qhd", probabilities, sequence_block[2], preferred_element_type=jnp.float32
        )
        return context.reshape(seq_len, inner_width).astype(jnp.bfloat16)

    stacked = lax.map(one_sequence, jnp.arange(row_count // seq_len, dtype=jnp.int32))
    return stacked.reshape(row_count, inner_width)


def on_device(tokens, pre_gain, input_weight, output_weight, position_bias, post_gain):
    rows_all, gain_all = (
        lax.all_gather(tokens, "mp", axis=1, tiled=True),
        lax.all_gather(pre_gain, "mp", axis=0, tiled=True),
    )
    widened = rows_all.astype(jnp.float32)
    inverse_rms = lax.rsqrt(jnp.mean(widened * widened, axis=1, keepdims=True) + epsilon)
    normed_in = (widened * inverse_rms * gain_all.astype(jnp.float32)).astype(jnp.bfloat16)
    feature_count = tokens.shape[1]
    projected = jnp.einsum(
        "td,kdi->kti",
        normed_in,
        lax.all_gather(input_weight, "dp", axis=1, tiled=True),
        preferred_element_type=jnp.float32,
    )
    context = attend_all(projected.astype(jnp.bfloat16), position_bias)
    partial_value = jnp.dot(
        context,
        lax.all_gather(output_weight, "dp", axis=1, tiled=True),
        preferred_element_type=jnp.float32,
    )
    attention_out = lax.psum_scatter(
        partial_value.astype(jnp.bfloat16), "mp", scatter_dimension=1, tiled=True
    ).astype(jnp.float32)
    stream = (tokens.astype(jnp.float32) + attention_out).astype(jnp.bfloat16)
    restored = lax.optimization_barrier(stream).astype(jnp.float32)
    squares = lax.psum(jnp.sum(restored * restored, axis=1), "mp")
    post_rms = lax.rsqrt(squares[:, None] / (feature_count * lax.axis_size("mp")) + epsilon)
    normed = (restored * post_rms * post_gain.astype(jnp.float32)).astype(jnp.bfloat16)
    return (stream, normed)


def solution(mesh):
    return jax.shard_map(
        on_device,
        mesh=mesh,
        in_specs=(
            P("dp", "mp"),
            P("mp"),
            P(None, "dp", "mp"),
            P("mp", "dp"),
            P("mp", None, None),
            P("mp"),
        ),
        out_specs=(P("dp", "mp"), P("dp", "mp")),
        check_vma=False,
    )
```

profile of v0, /device:TPU:0, one launch (start us, length us, event | category | flops | bytes accessed | tf_op | source)
XLA Modules:
  0.0 123.4 jit_solution(2190378064825369234)
XLA Ops:
  7.2 0.0 all-gather.4.cloned.1.call-start
  7.2 0.7 all-gather.4.cloned.1.call-update
  7.9 0.0 all-gather.6.cloned.1.call-start
  7.9 1.7 %copy.11 = bf16[3,128,256]{1,2,0:T(8,128)(2,1)} copy(bf16[3,128,256]{2,1,0:T(8,128)(2,1)} %param.8) | data formatting | bytes 393216 | tf_op args[2]
  9.7 0.0 all-gather.6.cloned.1.call-update
  9.7 0.0 reduce-scatter.2.cloned.1.call-start
  9.8 0.7 reshape.34
  10.4 12.6 %all-gather = bf16[4,1,256]{2,1,0:T(2,128)(2,1)S(1)} all-gather(bf16[1,1,256]{2,1,0:T(2,128)(2,1)S(1)} %reshape.34), channel_id=1, replica_groups=mesh['dp'=8,'mp'=4] {'mp'}, dimensions={0}, use_global_device_ids=true | all-gather | bytes 2560 | tf_op jit(solution)/shard_map/all_gather | solution.py:45
  23.1 2.8 %copy.12 = bf16[4,512,512]{1,2,0:T(8,128)(2,1)S(1)} copy(bf16[4,512,512]{2,1,0:T(8,128)(2,1)} %param.10) | data formatting | bytes 4194304 | tf_op args[4]
  25.9 10.0 %all_gather.15 = bf16[256,1024]{1,0:T(8,128)(2,1)S(1)} all-gather(bf16[256,128]{1,0:T(8,128)(2,1)S(1)} %copy-done.2), channel_id=1, replica_groups=mesh['dp'=8,'mp'=4] {'dp'}, dimensions={1}, use_global_device_ids=true | all-gather | bytes 589824 | tf_op jit(solution)/shard_map/all_gather | solution.py:60
  35.9 6.2 %all-gather.4.cloned.1.call-done = bf16[512,1024]{1,0:T(8,128)(2,1)} async-done(((bf16[512,256]{1,0:T(8,128)(2,1)}), bf16[512,1024]{1,0:T(8,128)(2,1)}) %all-gather.4.cloned.1.call-update) | async-done | bytes 1048592 | tf_op jit(solution)/shard_map/all_gather | solution.py:44
  42.1 1.5 %fusion.2 = f32[512]{0:T(512)S(1)} fusion(bf16[512,1024]{1,0:T(8,128)(2,1)} %all-gather.4.cloned.1.call-done), kind=kLoop, calls=%fused_computation.7 | loop fusion | flops 1572352 | bytes 1050624 | tf_op jit(solution)/shard_map/reduce_sum | solution.py:48
  43.6 25.1 %all-gather.6.cloned.1.call-done = bf16[3,1024,256]{1,2,0:T(8,128)(2,1)} async-done(((bf16[3,128,256]{1,2,0:T(8,128)(2,1)}), bf16[3,1024,256]{1,2,0:T(8,128)(2,1)}) %all-gather.6.cloned.1.call-update) | async-done | bytes 1572880 | tf_op jit(solution)/shard_map/all_gather | solution.py:54
  68.7 2.8 %fusion.6 = bf16[3,512,256]{1,2,0:T(8,128)(2,1)S(1)} fusion(bf16[3,1024,256]{1,2,0:T(8,128)(2,1)} %all-gather.6.cloned.1.call-done, bf16[512,1024]{1,0:T(8,128)(2,1)} %all-gather.4.cloned.1.call-done, f32[1024]{0:T(1024)S(1)} %bitcast.26, f32[512]{0:T(512)S(1)} %add_rsqrt_fusion.1), kind=kOutput, calls=%fused_computation.13 | convolution fusion | flops 807796736 | bytes 3414016 | tf_op jit(solution)/shard_map/td,kdi->kti/dot_general | solution.py:51
  71.5 0.8 fusion.18
  72.3 1.5 %fusion.19 = f32[4,512]{1,0:T(4,128)S(1)} fusion(bf16[4,512,512]{1,2,0:T(8,128)(2,1)S(1)} %copy.12, bf16[512,4,64]{0,2,1:T(8,128)(2,1)S(1)} %bitcast.23, bf16[512,4,64]{0,2,1:T(8,128)(2,1)S(1)} %bitcast.21), kind=kOutput, calls=%fused_computation.29 | convolution fusion | flops 138412544 | bytes 2629632 | tf_op jit(solution)/shard_map/while/body/eval_jaxpr/sub | solution.py:31
  73.8 2.9 %fusion.7 = bf16[4,64,512]{2,1,0:T(8,128)(2,1)S(1)} fusion(bf16[512,4,64]{0,2,1:T(8,128)(2,1)} %bitcast.25, f32[4,512]{1,0:T(4,128)S(1)} %fusion.19, bf16[4,512,512]{1,2,0:T(8,128)(2,1)S(1)} %copy.12, bf16[512,4,64]{0,2,1:T(8,128)(2,1)S(1)} %bitcast.24, bf16[512,4,64]{0,2,1:T(8,128)(2,1)S(1)} %bitcast.22), kind=kOutput, calls=%fused_computation.14 | convolution fusion | flops 273811968 | bytes 3153920 | tf_op jit(solution)/shard_map/while/body/eval_jaxpr/hqk,khd->qhd/dot_general | solution.py:33
  76.6 1.4 %convolution_convert_fusion = bf16[512,1024]{1,0:T(8,128)(2,1)} fusion(bf16[512,256]{0,1:T(8,128)(2,1)S(1)} %bitcast.20, bf16[256,1024]{1,0:T(8,128)(2,1)S(1)} %all_gather.15), kind=kOutput, calls=%fused_computation.11 | convolution fusion | flops 268959744 | bytes 1835008 | tf_op jit(solution)/shard_map/dot_general | solution.py:58
  78.1 0.0 reduce-scatter.2.cloned.1.call-update
  78.1 27.4 %reduce-scatter.2.cloned.1.call-done = bf16[512,256]{1,0:T(8,128)(2,1)} async-done(((bf16[512,1024]{1,0:T(8,128)(2,1)}), bf16[512,256]{1,0:T(8,128)(2,1)}) %reduce-scatter.2.cloned.1.call-update) | async-done | bytes 262160 | tf_op jit(solution)/shard_map/reduce_scatter | solution.py:63
  105.6 1.0 add_convert_fusion
  106.6 0.1 fusion.12
  106.7 9.3 %psum.7 = f32[512]{0:T(512)S(1)} all-reduce(f32[512]{0:T(512)S(1)} %fusion.12), channel_id=1, replica_groups=mesh['dp'=8,'mp'=4] {'mp'}, use_global_device_ids=true, to_apply=%region_5.6 | all-reduce | flops 512 | bytes 4096 | tf_op jit(solution)/shard_map/psum | solution.py:68
  116.0 0.8 fusion.14
  (12 shorter events, 0.0 us)
Async XLA Ops:
  7.2 35.0 %all-gather.4.cloned.1.call-start = ((), (), s32[]{:S(2)}) async-start(), calls=%async_computation.1 | async-start | bytes 1310720 | tf_op jit(solution)/shard_map/all_gather | solution.py:44
  7.9 60.8 %all-gather.6.cloned.1.call-start = ((), (), s32[]{:S(2)}) async-start(), calls=%async_computation.2 | async-start | bytes 1769472 | tf_op jit(solution)/shard_map/all_gather | solution.py:54
  9.7 95.8 %reduce-scatter.2.cloned.1.call-start = ((), (), s32[]{:S(2)}) async-start(), calls=%async_computation.3 | async-start | bytes 1310720 | tf_op jit(solution)/shard_map/reduce_scatter | solution.py:63
  23.1 2.8 %copy-start.2 = (bf16[256,128]{1,0:T(8,128)(2,1)S(1)}, bf16[256,128]{1,0:T(8,128)(2,1)}, u32[]{:S(2)}) copy-start(bf16[256,128]{1,0:T(8,128)(2,1)} %param.9) | copy-start | bytes 196612
  76.6 1.5 %copy-start.3 = (bf16[256]{0:T(256)(128)(2,1)S(1)}, bf16[256]{0:T(256)(128)(2,1)}, u32[]{:S(2)}) copy-start(bf16[256]{0:T(256)(128)(2,1)} %param.11) | copy-start | bytes 1540
  76.6 28.9 %copy-start.1 = (bf16[512,256]{1,0:T(8,128)(2,1)S(1)}, bf16[512,256]{1,0:T(8,128)(2,1)}, u32[]{:S(2)}) copy-start(bf16[512,256]{1,0:T(8,128)(2,1)} %param.6) | copy-start | bytes 786436
  106.6 10.3 %copy-start = (bf16[512,256]{1,0:T(8,128)(2,1)}, bf16[512,256]{1,0:T(8,128)(2,1)S(1)}, u32[]{:S(2)}) copy-start(bf16[512,256]{1,0:T(8,128)(2,1)S(1)} %add_convert_fusion) | copy-start | bytes 786436
Sparse Core Ops, SparseCore 0:
  9.5 32.5 all-gather.3
  44.6 24.0 all-gather.5
  78.2 27.2 reduce-scatter.1
where the time goes:
time: 124 us; the launch traced here: 123 us
  waiting for transfers between devices  59.4 us (48%)
  blocking collectives  31.9 us (26%)
  between operations  13.8 us (11%)
  matrix products  8.6 us (7%)
  local copies, waits for them, and re-layouts  6 us (5%)
  other arithmetic  3.54 us (3%)
    reduce_scatter x1, waiting for transfers between devices, on_device(): lax.psum_scatter(partial_value.astype(jnp.bfloat16), 'mp', scatter_dimens...  27.4 us
    all_gather x1, waiting for transfers between devices, on_device(): lax.all_gather(input_weight, 'dp', axis=1, tiled=True)  25.1 us
    all_gather x1, blocking collectives, on_device(): lax.all_gather(pre_gain, 'mp', axis=0, tiled=True)  12.6 us
    all_gather x1, blocking collectives, on_device(): lax.all_gather(output_weight, 'dp', axis=1, tiled=True)  9.99 us
    psum x1, blocking collectives, on_device(): squares = lax.psum(jnp.sum(restored * restored, axis=1), 'mp')  9.28 us
    all_gather x1, waiting for transfers between devices, on_device(): lax.all_gather(tokens, 'mp', axis=1, tiled=True)  6.23 us
    unnamed x11, local copies, waits for them, and re-layouts  5.24 us
    dot_general x1, matrix products, one_sequence(): jnp.einsum('hqk,khd->qhd', probabilities, sequence_block[2], preferred_el...  2.86 us
  transfers between devices with their start and end apart: 3, of which 3 were waited for; matrix products, arithmetic and copies ran while one was open for 5% of the time, Pallas kernels for 0%

commit v1 on v0

--- a/solution.py
+++ b/solution.py
@@ -48,11 +48,9 @@
     inverse_rms = lax.rsqrt(jnp.mean(widened * widened, axis=1, keepdims=True) + epsilon)
     normed_in = (widened * inverse_rms * gain_all.astype(jnp.float32)).astype(jnp.bfloat16)
     feature_count = tokens.shape[1]
+    outputs_apply = lambda m: jnp.concatenate(lax.all_gather(m, "dp"), axis=1)
     projected = jnp.einsum(
-        "td,kdi->kti",
-        normed_in,
-        lax.all_gather(input_weight, "dp", axis=1, tiled=True),
-        preferred_element_type=jnp.float32,
+        "td,kdi->kti", normed_in, outputs_apply(input_weight), preferred_element_type=jnp.float32
     )
     context = attend_all(projected.astype(jnp.bfloat16), position_bias)
     partial_value = jnp.dot(

time: 124 us -> 127 us (1.024)
  local copies, waits for them, and re-layouts: 6 us -> 9.66 us
    reshape x0 -> x1, local copies, waits for them, and re-layouts: none -> 2.06 us  [on_device(): outputs_apply = lambda m: jnp.concatenate(lax.all_gather(m, 'dp'), axis=1)]
    all_gather x0 -> x1, local copies, waits for them, and re-layouts: none -> 1.99 us  [on_device(): outputs_apply = lambda m: jnp.concatenate(lax.all_gather(m, 'dp'), axis=1)]
    unnamed x11 -> x12, local copies, waits for them, and re-layouts: 5.24 us -> 4.86 us
where the time goes in v1:
time: 127 us
  waiting for transfers between devices  59.2 us (47%)
  blocking collectives  31.9 us (25%)
  between operations  13.8 us (11%)
  local copies, waits for them, and re-layouts  9.66 us (8%)
  matrix products  8.74 us (7%)
  other arithmetic  3.54 us (3%)
    reduce_scatter x1, waiting for transfers between devices, on_device(): lax.psum_scatter(partial_value.astype(jnp.bfloat16), 'mp', scatter_dimens...  27.4 us
    all_gather x1, waiting for transfers between devices, on_device(): outputs_apply = lambda m: jnp.concatenate(lax.all_gather(m, 'dp'), axis=1)  24.3 us
    all_gather x1, blocking collectives, on_device(): lax.all_gather(pre_gain, 'mp', axis=0, tiled=True)  12.6 us
    all_gather x1, blocking collectives, on_device(): lax.all_gather(output_weight, 'dp', axis=1, tiled=True)  9.97 us
    psum x1, blocking collectives, on_device(): squares = lax.psum(jnp.sum(restored * restored, axis=1), 'mp')  9.27 us
    all_gather x1, waiting for transfers between devices, on_device(): lax.all_gather(tokens, 'mp', axis=1, tiled=True)  6.07 us
    unnamed x12, local copies, waits for them, and re-layouts  4.86 us
    dot_general x1, matrix products, on_device(): jnp.einsum('td,kdi->kti', normed_in, outputs_apply(input_weight), preferr...  2.96 us
  transfers between devices with their start and end apart: 3, of which 3 were waited for; matrix products, arithmetic and copies ran while one was open for 5% of the time, Pallas kernels for 0%

profile of v1, /device:TPU:0, one launch (start us, length us, event | category | flops | bytes accessed | tf_op | source)
XLA Modules:
  0.0 126.9 jit_solution(13989687125198992293)
XLA Ops:
  7.2 0.0 all-gather.5.cloned.1.call-start
  7.2 0.7 all-gather.5.cloned.1.call-update
  7.9 0.0 all-gather.7.cloned.1.call-start
  7.9 0.7 all-gather.7.cloned.1.call-update
  8.6 0.0 reduce-scatter.2.cloned.1.call-start
  8.7 0.7 reshape.43
  9.4 12.6 %all-gather.1 = bf16[4,1,256]{2,1,0:T(2,128)(2,1)S(1)} all-gather(bf16[1,1,256]{2,1,0:T(2,128)(2,1)S(1)} %reshape.43), channel_id=1, replica_groups=mesh['dp'=8,'mp'=4] {'mp'}, dimensions={0}, use_global_device_ids=true | all-gather | bytes 2560 | tf_op jit(solution)/shard_map/all_gather | solution.py:45
  22.0 4.2 %copy.12 = bf16[4,512,512]{1,2,0:T(8,128)(2,1)} copy(bf16[4,512,512]{2,1,0:T(8,128)(2,1)} %param.10) | data formatting | bytes 4194304 | tf_op args[4]
  26.2 10.0 %all_gather.19 = bf16[256,1024]{1,0:T(8,128)(2,1)S(1)} all-gather(bf16[256,128]{1,0:T(8,128)(2,1)S(1)} %copy-done.3), channel_id=1, replica_groups=mesh['dp'=8,'mp'=4] {'dp'}, dimensions={1}, use_global_device_ids=true | all-gather | bytes 589824 | tf_op jit(solution)/shard_map/all_gather | solution.py:58
  36.2 6.1 %all-gather.5.cloned.1.call-done = bf16[512,1024]{1,0:T(8,128)(2,1)} async-done(((bf16[512,256]{1,0:T(8,128)(2,1)}), bf16[512,1024]{1,0:T(8,128)(2,1)}) %all-gather.5.cloned.1.call-update) | async-done | bytes 1048592 | tf_op jit(solution)/shard_map/all_gather | solution.py:44
  42.2 1.5 %fusion.2 = f32[512]{0:T(512)S(1)} fusion(bf16[512,1024]{1,0:T(8,128)(2,1)} %all-gather.5.cloned.1.call-done), kind=kLoop, calls=%fused_computation.7 | loop fusion | flops 1572352 | bytes 1050624 | tf_op jit(solution)/shard_map/reduce_sum | solution.py:48
  43.7 24.3 %all-gather.7.cloned.1.call-done = bf16[24,128,256]{2,1,0:T(8,128)(2,1)} async-done(((bf16[3,128,256]{2,1,0:T(8,128)(2,1)}), bf16[24,128,256]{2,1,0:T(8,128)(2,1)}) %all-gather.7.cloned.1.call-update) | async-done | bytes 1572880 | tf_op jit(solution)/shard_map/all_gather | solution.py:51
  68.0 2.0 %copy.11 = bf16[8,3,128,256]{2,0,3,1:T(8,128)(2,1)S(1)} copy(bf16[8,3,128,256]{3,2,1,0:T(8,128)(2,1)} %bitcast.27) | data formatting | bytes 3145728 | tf_op jit(solution)/shard_map/all_gather | solution.py:51
  70.0 2.1 %reshape.41 = bf16[3,1024,256]{1,2,0:T(8,128)(2,1)} reshape(bf16[3,8,128,256]{2,1,3,0:T(8,128)(2,1)S(1)} %bitcast.26) | data formatting | bytes 3145728 | tf_op jit(solution)/shard_map/reshape | solution.py:51
  72.1 3.0 %fusion.6 = bf16[3,512,256]{1,2,0:T(8,128)(2,1)S(1)} fusion(bf16[3,1024,256]{1,2,0:T(8,128)(2,1)} %reshape.41, bf16[512,1024]{1,0:T(8,128)(2,1)} %all-gather.5.cloned.1.call-done, f32[1024]{0:T(1024)S(1)} %bitcast.34, f32[512]{0:T(512)S(1)} %add_rsqrt_fusion.1), kind=kOutput, calls=%fused_computation.13 | convolution fusion | flops 807796736 | bytes 3414016 | tf_op jit(solution)/shard_map/td,kdi->kti/dot_general | solution.py:52
  75.0 0.8 fusion.18
  75.8 1.5 %fusion.19 = f32[4,512]{1,0:T(4,128)S(1)} fusion(bf16[4,512,512]{1,2,0:T(8,128)(2,1)S(1)} %copy-done.1, bf16[512,4,64]{0,2,1:T(8,128)(2,1)S(1)} %bitcast.31, bf16[512,4,64]{0,2,1:T(8,128)(2,1)S(1)} %bitcast.29), kind=kOutput, calls=%fused_computation.29 | convolution fusion | flops 138412544 | bytes 2629632 | tf_op jit(solution)/shard_map/while/body/eval_jaxpr/sub | solution.py:31
  77.3 2.9 %fusion.7 = bf16[4,64,512]{2,1,0:T(8,128)(2,1)S(1)} fusion(bf16[512,4,64]{0,2,1:T(8,128)(2,1)} %bitcast.33, f32[4,512]{1,0:T(4,128)S(1)} %fusion.19, bf16[4,512,512]{1,2,0:T(8,128)(2,1)S(1)} %copy-done.1, bf16[512,4,64]{0,2,1:T(8,128)(2,1)S(1)} %bitcast.32, bf16[512,4,64]{0,2,1:T(8,128)(2,1)S(1)} %bitcast.30), kind=kOutput, calls=%fused_computation.14 | convolution fusion | flops 273811968 | bytes 3153920 | tf_op jit(solution)/shard_map/while/body/eval_jaxpr/hqk,khd->qhd/dot_general | solution.py:33
  80.2 1.4 %convolution_convert_fusion = bf16[512,1024]{1,0:T(8,128)(2,1)} fusion(bf16[512,256]{0,1:T(8,128)(2,1)S(1)} %bitcast.28, bf16[256,1024]{1,0:T(8,128)(2,1)S(1)} %all_gather.19), kind=kOutput, calls=%fused_computation.11 | convolution fusion | flops 268959744 | bytes 1835008 | tf_op jit(solution)/shard_map/dot_general | solution.py:56
  81.7 27.4 %reduce-scatter.2.cloned.1.call-done = bf16[512,256]{1,0:T(8,128)(2,1)} async-done(((bf16[512,1024]{1,0:T(8,128)(2,1)}), bf16[512,256]{1,0:T(8,128)(2,1)}) %reduce-scatter.2.cloned.1.call-update) | async-done | bytes 262160 | tf_op jit(solution)/shard_map/reduce_scatter | solution.py:61
  109.1 1.0 add_convert_fusion
  110.1 0.1 fusion.12
  110.3 9.3 %psum.7 = f32[512]{0:T(512)S(1)} all-reduce(f32[512]{0:T(512)S(1)} %fusion.12), channel_id=1, replica_groups=mesh['dp'=8,'mp'=4] {'mp'}, use_global_device_ids=true, to_apply=%region_5.6 | all-reduce | flops 512 | bytes 4096 | tf_op jit(solution)/shard_map/psum | solution.py:66
  119.5 0.8 fusion.14
  (15 shorter events, 0.1 us)
Async XLA Ops:
  7.2 35.1 %all-gather.5.cloned.1.call-start = ((), (), s32[]{:S(2)}) async-start(), calls=%async_computation.1 | async-start | bytes 1310720 | tf_op jit(solution)/shard_map/all_gather | solution.py:44
  7.9 60.1 %all-gather.7.cloned.1.call-start = ((), (), s32[]{:S(2)}) async-start(), calls=%async_computation.3 | async-start | bytes 1769472 | tf_op jit(solution)/shard_map/all_gather | solution.py:51
  8.6 100.4 %reduce-scatter.2.cloned.1.call-start = ((), (), s32[]{:S(2)}) async-start(), calls=%async_computation.2 | async-start | bytes 1310720 | tf_op jit(solution)/shard_map/reduce_scatter | solution.py:61
  22.0 4.2 %copy-start.3 = (bf16[256,128]{1,0:T(8,128)(2,1)S(1)}, bf16[256,128]{1,0:T(8,128)(2,1)}, u32[]{:S(2)}) copy-start(bf16[256,128]{1,0:T(8,128)(2,1)} %param.9) | copy-start | bytes 196612
  72.1 3.7 %copy-start.1 = (bf16[4,512,512]{1,2,0:T(8,128)(2,1)S(1)}, bf16[4,512,512]{1,2,0:T(8,128)(2,1)}, u32[]{:S(2)}) copy-start(bf16[4,512,512]{1,2,0:T(8,128)(2,1)} %copy.12) | copy-start | bytes 6291460
  80.1 1.5 %copy-start.4 = (bf16[256]{0:T(256)(128)(2,1)S(1)}, bf16[256]{0:T(256)(128)(2,1)}, u32[]{:S(2)}) copy-start(bf16[256]{0:T(256)(128)(2,1)} %param.11) | copy-start | bytes 1540
  80.1 28.9 %copy-start.2 = (bf16[512,256]{1,0:T(8,128)(2,1)S(1)}, bf16[512,256]{1,0:T(8,128)(2,1)}, u32[]{:S(2)}) copy-start(bf16[512,256]{1,0:T(8,128)(2,1)} %param.6) | copy-start | bytes 786436
  110.1 10.3 %copy-start = (bf16[512,256]{1,0:T(8,128)(2,1)}, bf16[512,256]{1,0:T(8,128)(2,1)S(1)}, u32[]{:S(2)}) copy-start(bf16[512,256]{1,0:T(8,128)(2,1)S(1)} %add_convert_fusion) | copy-start | bytes 786436
Sparse Core Ops, SparseCore 0:
  9.5 32.6 all-gather.4
  44.1 23.8 all-gather.6
  81.8 27.2 reduce-scatter.1
